TPU v7x, 32 devices: a whole 2x2x4 slice. The times are simulated.
32 devices in a mesh: dp: 4 (over y, x), expert: 8 (over z, core).
Axes of the slice: x: 2, y: 2, z: 4, core: 2. Of those that a mesh axis runs over, the one named last changes fastest.
Arguments:
- grad_out: bfloat16 [4096, 3072], P(('dp', 'expert')), may hold values from -6 to 6
- expert_ids: int32 [4096, 2], P(('dp', 'expert')), may hold values from 0 to 7, all different within a row; in each aligned block of 128 rows (0 to 127, 128 to 255, ...) at most 36 rows name the same one
- down_weight: bfloat16 [8, 1024, 3072], P('expert'), may hold values from -0.109375 to 0.109375
- history_grad: float32 [8, 8], replicated, may hold values from 0.5 to 3
- history_hidden: float32 [8, 8], replicated, may hold values from 0.5 to 3
Outputs:
- hidden_scaled: bfloat16 [4, 8, 288, 1024], P('dp', 'expert')
- new_history_grad: float32 [8, 8], replicated
- new_history_hidden: float32 [8, 8], replicated
Inputs may be any that keep to these rules, and one draw needn't show every extreme that they name: `expert_ids`: each row names 2 different experts; among the 128 rows of one device no expert is named more than 36 times, a bound that some block reaches in some devices.
All inputs are finite; a program needn't handle non-finite values.
Results may differ from a plain program's by a relative error of at most 0.0045.
Values may be sent and summed in bfloat16 or wider, within the bound.
A program may use at most 128 MiB of HBM per device.

v0:
```python
import jax
import jax.numpy as jnp
from jax import lax
from jax.sharding import PartitionSpec as P


def per_device(grad_out, expert_ids, down_weight, history_grad, history_hidden):
    tok_rows = grad_out.shape[0]
    experts = history_grad.shape[1]
    slices = lax.axis_size("expert") // experts
    capacity = tok_rows * 9 // 32
    flat_ids = expert_ids.reshape(-1)
    onehot = (flat_ids[:, None] == jnp.arange(experts, dtype=jnp.int32)[None, :]).astype(jnp.int32)
    before = jnp.cumsum(onehot, axis=0) - onehot
    slot_index = jnp.sum(before * onehot, axis=1)
    target = flat_ids * capacity + slot_index
    matches = (jnp.arange(experts * capacity, dtype=jnp.int32)[:, None] == target[None, :]).astype(
        jnp.int32
    )
    dispatch = jnp.sum(matches.reshape(experts * capacity, tok_rows, 2), axis=2).astype(
        jnp.bfloat16
    )
    gathered = jnp.dot(dispatch, grad_out, preferred_element_type=jnp.float32)
    scale_in = 1.0 / jnp.max(history_grad, axis=0)
    scale_hidden = 1.0 / jnp.max(history_hidden, axis=0)
    quantized = jnp.clip(
        gathered.reshape(experts, capacity, -1) * scale_in[:, None, None], -1.0, 1.0
    ).astype(jnp.bfloat16)
    own_index = lax.axis_index("expert")
    own_expert = own_index // slices
    chosen = jnp.arange(experts, dtype=jnp.int32) == own_expert
    own_scale_in = jnp.sum(jnp.where(chosen, scale_in, 0.0))
    own_scale_hidden = jnp.sum(jnp.where(chosen, scale_hidden, 0.0))
    routed = jnp.max(onehot.reshape(tok_rows, 2, experts), axis=1) > 0
    row_peak = jnp.max(jnp.abs(grad_out.astype(jnp.float32)), axis=1)
    grad_peak = jnp.max(jnp.where(routed, row_peak[:, None], 0.0), axis=0)
    weight_block = down_weight[0]
    outgoing = jnp.repeat(quantized, slices, axis=0)
    received = lax.all_to_all(outgoing, "expert", split_axis=0, concat_axis=0, tiled=True)
    product = jnp.einsum("sic,uc->siu", received, weight_block, preferred_element_type=jnp.float32)
    hidden = product / own_scale_in
    hidden_peak = jnp.max(jnp.abs(hidden))
    hidden_vec = jnp.where(chosen, hidden_peak, 0.0)
    grad_amax, hidden_amax = lax.pmax((grad_peak, hidden_vec), ("dp", "expert"))
    scaled = jnp.clip(hidden * own_scale_hidden, -1.0, 1.0).astype(jnp.bfloat16)
    hidden_scaled = scaled.reshape(1, 1, -1, scaled.shape[2])
    new_history_grad = jnp.concatenate([history_grad[1:], grad_amax[None, :]], axis=0)
    new_history_hidden = jnp.concatenate([history_hidden[1:], hidden_amax[None, :]], axis=0)
    return (hidden_scaled, new_history_grad, new_history_hidden)


def solution(mesh):
    in_specs = (
        P(("dp", "expert"), None),
        P(("dp", "expert"), None),
        P("expert", None, None),
        P(),
        P(),
    )
    out_specs = (P("dp", "expert", None, None), P(), P())
    return jax.shard_map(
        per_device, mesh=mesh, in_specs=in_specs, out_specs=out_specs, check_vma=False
    )
```

profile of v0, /device:TPU:0, one launch (start us, length us, event | category | flops | bytes accessed | tf_op | source)
XLA Modules:
  0.0 111.7 jit_solution(3754334476926324953)
XLA Ops:
  0.6 0.8 copy.20
  1.4 0.1 eq.57
  1.6 0.1 eq.53
  1.7 0.6 reduce-window.6
  2.3 0.2 slice_reduce_fusion
  2.6 0.1 fusion.8
  2.7 0.1 reduce_sum.39
  2.8 0.1 copy.22
  2.9 0.7 multiply_add_fusion
  3.6 1.7 %fusion.5 = f32[288,3072]{1,0:T(8,128)S(1)} fusion(bf16[128,3072]{1,0:T(8,128)(2,1)} %param.5, s32[288,128]{1,0:T(8,128)S(1)} %convert_reduce_fusion), kind=kOutput, calls=%fused_computation.9 | convolution fusion | flops 226529280 | bytes 4472832 | tf_op jit(solution)/shard_map/dot_general | solution.py:23
  5.4 0.0 copy-start.1
  5.4 2.1 %reshape.61 = f32[8,36,3072]{2,1,0:T(8,128)} reshape(f32[288,3072]{1,0:T(8,128)S(1)} %fusion.5) | data formatting | bytes 7077888 | tf_op jit(solution)/shard_map/reshape | solution.py:27
  7.4 0.0 copy-done.1
  7.5 0.6 select_reduce_fusion.1
  8.1 3.8 %clamp_convert_fusion = bf16[8,36,3072]{2,1,0:T(8,128)(2,1)} fusion(f32[8,36,3072]{2,1,0:T(8,128)} %reshape.61, f32[8]{0:T(128)S(1)} %get-tuple-element.6), kind=kLoop, calls=%fused_computation.2 | loop fusion | flops 2654208 | bytes 5308448 | tf_op jit(solution)/shard_map/convert_element_type | solution.py:28
  11.9 0.0 copy-start.2
  11.9 0.0 copy-start.3
  11.9 0.0 copy-start
  11.9 6.5 %all-to-all-start = ((bf16[8,36,3072]{2,1,0:T(8,128)(2,1)}), bf16[8,36,3072]{2,1,0:T(8,128)(2,1)S(1)}, u32[]{:S(2)}, u32[]{:S(2)}) async-start(bf16[8,36,3072]{2,1,0:T(8,128)(2,1)} %clamp_convert_fusion), calls=%async_computation | async-start | bytes 3932160 | tf_op jit(solution)/shard_map/all_to_all | solution.py:39
  18.4 0.0 copy-done.2
  18.5 0.0 copy-done.3
  18.5 0.0 copy-done
  18.5 0.2 abs_reduce_fusion
  18.7 0.1 select_reduce_fusion
  18.8 0.6 fusion.10
  19.4 45.2 %all-to-all-done = bf16[8,36,3072]{2,1,0:T(8,128)(2,1)S(1)} async-done(((bf16[8,36,3072]{2,1,0:T(8,128)(2,1)}), bf16[8,36,3072]{2,1,0:T(8,128)(2,1)S(1)}, u32[]{:S(2)}, u32[]{:S(2)}) %all-to-all-start) | async-done | bytes 1769504 | tf_op jit(solution)/shard_map/all_to_all | solution.py:39
  64.6 7.1 %abs_reduce_fusion.1 = (f32[]{:T(128)}, bf16[8,36,1024]{2,1,0:T(8,128)(2,1)S(1)}) fusion(f32[]{:T(128)} %fusion.10, f32[]{:T(128)} %get-tuple-element.5, bf16[8,36,3072]{2,1,0:T(8,128)(2,1)S(1)} %all-to-all-done, bf16[1,1024,3072]{2,1,0:T(8,128)(2,1)} %param.7), kind=kOutput, calls=%fused_computation.4 | convolution fusion | flops 1813708800 | bytes 8650764 | tf_op jit(solution)/shard_map/sic,uc->siu/dot_general | solution.py:40
  71.7 0.6 select_bitcast_fusion
  72.4 0.9 reshape.62
  73.3 37.8 %all-reduce = (f32[1,8]{1,0:T(1,128)S(1)}, f32[1,8]{1,0:T(1,128)S(1)}) all-reduce(f32[1,8]{1,0:T(1,128)S(1)} %bitcast.21, f32[1,8]{1,0:T(1,128)S(1)} %select_bitcast_fusion), channel_id=1, replica_groups=mesh['dp'=4,'expert'=8] {'dp','expert'}, use_global_device_ids=true, to_apply=%region_11.12 | all-reduce | flops 16 | bytes 128 | tf_op jit(solution)/shard_map/pmax | solution.py:44
  111.1 0.6 pad_maximum_fusion
  (9 shorter events, 0.1 us)
Async XLA Ops:
  5.4 2.1 %copy-start.1 = (f32[8,8]{1,0:T(8,128)S(1)}, f32[8,8]{1,0:T(8,128)}, u32[]{:S(2)}) copy-start(f32[8,8]{1,0:T(8,128)} %param.8) | copy-start | bytes 772
  11.9 6.5 %copy-start.2 = (f32[8,8]{1,0:T(8,128)S(1)}, f32[8,8]{1,0:T(8,128)}, u32[]{:S(2)}) copy-start(f32[8,8]{1,0:T(8,128)} %param.9) | copy-start | bytes 772
  11.9 6.5 %copy-start.3 = (s32[128,2]{0,1:T(2,128)S(1)}, s32[128,2]{0,1:T(2,128)}, u32[]{:S(2)}) copy-start(s32[128,2]{0,1:T(2,128)} %param.6) | copy-start | bytes 3076
  11.9 6.6 %copy-start = (bf16[128,3072]{1,0:T(8,128)(2,1)S(1)}, bf16[128,3072]{1,0:T(8,128)(2,1)}, u32[]{:S(2)}) copy-start(bf16[128,3072]{1,0:T(8,128)(2,1)} %param.5) | copy-start | bytes 2359300
  11.9 52.7 %all-to-all-start = ((bf16[8,36,3072]{2,1,0:T(8,128)(2,1)}), bf16[8,36,3072]{2,1,0:T(8,128)(2,1)S(1)}, u32[]{:S(2)}, u32[]{:S(2)}) async-start(bf16[8,36,3072]{2,1,0:T(8,128)(2,1)} %clamp_convert_fusion), calls=%async_computation | async-start | bytes 3932160 | tf_op jit(solution)/shard_map/all_to_all | solution.py:39
where the time goes:
time: 113 us; the launch traced here: 112 us
  waiting for transfers between devices  45.2 us (40%)
  blocking collectives  37.8 us (33%)
  matrix products  8.85 us (8%)
  other arithmetic  8.16 us (7%)
  starting transfers between devices  6.49 us (6%)
  local copies, waits for them, and re-layouts  4.51 us (4%)
    all_to_all x1, waiting for transfers between devices, per_device(): lax.all_to_all(outgoing, 'expert', split_axis=0, concat_axis=0, tiled=True)  45.2 us
    pmax x1, blocking collectives, per_device(): grad_amax, hidden_amax = lax.pmax((grad_peak, hidden_vec), ('dp', 'expert'))  37.8 us
    dot_general x1, matrix products, per_device(): jnp.einsum('sic,uc->siu', received, weight_block, preferred_element_type=...  7.11 us
    all_to_all x1, starting transfers between devices, per_device(): lax.all_to_all(outgoing, 'expert', split_axis=0, concat_axis=0, tiled=True)  6.49 us
    convert_element_type x1, other arithmetic, per_device(): quantized = jnp.clip(gathered.reshape(experts, capacity, -1) * scale_in[:...  3.85 us
  transfers between devices with their start and end apart: 1, of which 1 were waited for; matrix products, arithmetic and copies ran while one was open for 1% of the time, Pallas kernels for 0%

commit v1 on v0

v1 whole, which is shorter than its diff:
```python
import functools

import jax
import jax.numpy as jnp
from jax import lax
from jax.experimental import pallas as pl
from jax.experimental.pallas import tpu as pltpu
from jax.sharding import PartitionSpec as P

MESH = pl.DeviceIdType.MESH
LANES = 128


def flip_bits(q, k, count):
    out, bit = 0, 1
    while bit < count:
        a, b = (q // bit) % 2, (k // bit) % 2
        out = out + bit * (a + b - 2 * a * b)
        bit *= 2
    return out


def kernel(
    n_dp, n_exp, experts, capacity,
    grad_ref, ids_ref, hist_g_ref, hist_h_ref, weight_hbm,
    out_ref, new_g_ref, new_h_ref,
    weight, send, recv, slots, mine, folded, dp_in, ex_in,
    weight_sem, send_sem, recv_sem, dps_sem, dpr_sem, exs_sem, exr_sem,
):
    tokens = grad_ref.shape[0]
    slices = n_exp // experts
    chips = n_exp // 2
    my_dp, me = lax.axis_index("dp"), lax.axis_index("expert")
    q0, c0 = me // 2, me % 2
    partner = q0 * 2 + 1 - c0
    own = me // slices
    load = pltpu.make_async_copy(weight_hbm.at[0], weight, weight_sem)
    load.start()

    barrier = pltpu.get_barrier_semaphore()

    def greet_exp(j, x):
        pl.semaphore_signal(barrier, inc=1, device_id=(my_dp, (me + j) % n_exp), device_id_type=MESH)
        return x

    def greet_dp(j, x):
        pl.semaphore_signal(barrier, inc=1, device_id=((my_dp + j) % n_dp, me), device_id_type=MESH)
        return x

    lax.fori_loop(1, n_exp, greet_exp, 0)
    lax.fori_loop(1, n_dp, greet_dp, 0)

    lane = lax.broadcasted_iota(jnp.int32, (tokens, LANES), 1)
    ids = ids_ref[...]
    routed = (ids[:, 0:1] == lane) | (ids[:, 1:2] == lane)
    mask_t = jnp.where(routed, 1.0, 0.0).T
    row = lax.broadcasted_iota(jnp.int32, (tokens, tokens), 0)
    col = lax.broadcasted_iota(jnp.int32, (tokens, tokens), 1)
    earlier = jnp.where(row < col, 1.0, 0.0).astype(jnp.bfloat16)
    before = jnp.dot(mask_t.astype(jnp.bfloat16), earlier, preferred_element_type=jnp.float32)
    slots[...] = jnp.where(mask_t > 0.5, before, -1.0)
    scale_in = 1.0 / jnp.max(hist_g_ref[...], axis=0, keepdims=True)
    scale_hidden = 1.0 / jnp.max(hist_h_ref[...], axis=0, keepdims=True)
    which = lax.broadcasted_iota(jnp.int32, (1, experts), 1)

    def pick(values, e):
        return jnp.sum(jnp.where(which == e, values, 0.0), axis=1, keepdims=True)

    position = lax.broadcasted_iota(jnp.int32, (capacity, tokens), 0).astype(jnp.float32)

    def prepare(e):
        onehot = jnp.where(slots[pl.ds(e, 1), :] == position, 1.0, 0.0).astype(jnp.bfloat16)
        rows = jnp.dot(onehot, grad_ref[...], preferred_element_type=jnp.float32)
        send[e] = jnp.clip(rows * pick(scale_in, e), -1.0, 1.0).astype(jnp.bfloat16)

    def outgoing(d):
        return pltpu.make_async_remote_copy(
            src_ref=send.at[d // slices], dst_ref=recv.at[me],
            send_sem=send_sem.at[d], recv_sem=recv_sem.at[me],
            device_id=(my_dp, d), device_id_type=MESH,
        )

    def incoming(s):
        return pltpu.make_async_remote_copy(
            src_ref=send.at[0], dst_ref=recv.at[s],
            send_sem=send_sem.at[s], recv_sem=recv_sem.at[s],
            device_id=(my_dp, s), device_id_type=MESH,
        )

    def chip_of(j):
        k = jnp.where(j < 2, j, chips + 1 - j)
        if chips & (chips - 1) == 0:
            return flip_bits(q0, k, chips)
        return (q0 + k) % chips

    def source_of(j):
        if chips & (chips - 1) == 0:
            return chip_of(j)
        k = jnp.where(j < 2, j, chips + 1 - j)
        return (q0 + chips - k) % chips

    def prepare_pair(q):
        prepare(2 * q + c0)
        prepare(2 * q + 1 - c0)

    def send_pair(q):
        outgoing(2 * q + c0).start()
        outgoing(2 * q + 1 - c0).start()

    greeted = n_exp + n_dp - 2
    if slices == 1:
        prepare_pair(chip_of(jnp.int32(1)))
        pl.semaphore_wait(barrier, greeted)

        def step(j, x):
            prepare_pair(chip_of((j + 1) % chips))
            send_pair(chip_of(j))
            return x
    else:
        def fill(e, x):
            prepare(e)
            return x

        lax.fori_loop(0, experts, fill, 0)
        pl.semaphore_wait(barrier, greeted)

        def step(j, x):
            send_pair(chip_of(j))
            return x

    lax.fori_loop(1, chips, step, 0)
    outgoing(partner).start()

    row_peak = jnp.max(jnp.abs(grad_ref[...]).astype(jnp.float32), axis=1, keepdims=True)
    grad_peak = jnp.max(jnp.where(routed, row_peak, 0.0), axis=0, keepdims=True)

    back = 1.0 / pick(scale_in, own)
    own_hidden = pick(scale_hidden, own)
    load.wait()

    def multiply(block, s):
        product = lax.dot_general(
            block, weight[...], (((1,), (1,)), ((), ())), preferred_element_type=jnp.float32
        )
        hidden = product * back
        out_ref[s] = jnp.clip(hidden * own_hidden, -1.0, 1.0).astype(jnp.bfloat16)
        return jnp.max(jnp.max(jnp.abs(hidden), axis=0, keepdims=True), axis=1, keepdims=True)

    peak = multiply(send[own], me)

    def take(s, peak):
        incoming(s).wait_recv()
        return jnp.maximum(peak, multiply(recv[s], s))

    def take_step(i, peak):
        q = source_of(i // 2)
        c = (c0 + i % 2) % 2
        return take(2 * q + c, peak)

    peak = take(partner, peak)
    peak = lax.fori_loop(2, n_exp, take_step, peak)

    at = lax.broadcasted_iota(jnp.int32, (1, LANES), 1)
    hidden_peak = jnp.where(at == own, peak, 0.0)
    part = lax.broadcasted_iota(jnp.int32, (8, LANES), 0)
    mine[...] = jnp.where(part == 0, grad_peak, jnp.where(part == 1, hidden_peak, 0.0))

    def dp_copy(j, back_way):
        peer = (my_dp + (n_dp - j if back_way else j)) % n_dp
        slot = peer if back_way else my_dp
        return pltpu.make_async_remote_copy(
            src_ref=mine, dst_ref=dp_in.at[slot], send_sem=dps_sem.at[j], recv_sem=dpr_sem.at[slot],
            device_id=(peer, me), device_id_type=MESH,
        )

    def ex_copy(j, back_way):
        peer = (me + (n_exp - j if back_way else j)) % n_exp
        slot = peer if back_way else me
        return pltpu.make_async_remote_copy(
            src_ref=folded, dst_ref=ex_in.at[slot], send_sem=exs_sem.at[j], recv_sem=exr_sem.at[slot],
            device_id=(my_dp, peer), device_id_type=MESH,
        )

    for copy, count, source, target, buffer in (
        (dp_copy, n_dp, mine, folded, dp_in), (ex_copy, n_exp, folded, mine, ex_in)
    ):
        def start(j, x, copy=copy):
            copy(j, False).start()
            return x

        def fold(j, best, copy=copy, count=count, buffer=buffer):
            copy(j, True).wait_recv()
            at_slot = ((my_dp if copy is dp_copy else me) + count - j) % count
            return jnp.maximum(best, buffer[at_slot])

        def finish(j, x, copy=copy):
            copy(j, False).wait_send()
            return x

        lax.fori_loop(1, count, start, 0)
        best = lax.fori_loop(1, count, fold, source[...])
        lax.fori_loop(1, count, finish, 0)
        target[...] = best

    keep = hist_g_ref.shape[0] - 1
    new_g_ref[0:keep, :] = hist_g_ref[1:keep + 1, :]
    new_g_ref[keep:keep + 1, :] = best[0:1, 0:experts]
    new_h_ref[0:keep, :] = hist_h_ref[1:keep + 1, :]
    new_h_ref[keep:keep + 1, :] = best[1:2, 0:experts]

    def drain(j, x):
        outgoing((me + j) % n_exp).wait_send()
        return x

    lax.fori_loop(1, n_exp, drain, 0)


def per_device(grad_out, expert_ids, down_weight, history_grad, history_hidden):
    tokens, width = grad_out.shape
    experts = history_grad.shape[1]
    n_dp, n_exp = lax.axis_size("dp"), lax.axis_size("expert")
    capacity = tokens * 9 // 32
    units = down_weight.shape[1]
    vmem = pl.BlockSpec(memory_space=pltpu.VMEM)
    dma = pltpu.SemaphoreType.DMA
    out, new_g, new_h = pl.pallas_call(
        functools.partial(kernel, n_dp, n_exp, experts, capacity),
        out_shape=(
            jax.ShapeDtypeStruct((n_exp, capacity, units), jnp.bfloat16),
            jax.ShapeDtypeStruct(history_grad.shape, jnp.float32),
            jax.ShapeDtypeStruct(history_hidden.shape, jnp.float32),
        ),
        in_specs=[vmem, vmem, vmem, vmem, pl.BlockSpec(memory_space=pl.ANY)],
        out_specs=(vmem, vmem, vmem),
        scratch_shapes=[
            pltpu.VMEM((units, width), jnp.bfloat16),
            pltpu.VMEM((experts, capacity, width), jnp.bfloat16),
            pltpu.VMEM((n_exp, capacity, width), jnp.bfloat16),
            pltpu.VMEM((LANES, tokens), jnp.float32),
            pltpu.VMEM((8, LANES), jnp.float32),
            pltpu.VMEM((8, LANES), jnp.float32),
            pltpu.VMEM((n_dp, 8, LANES), jnp.float32),
            pltpu.VMEM((n_exp, 8, LANES), jnp.float32),
            dma, dma((n_exp,)), dma((n_exp,)), dma((n_dp,)), dma((n_dp,)), dma((n_exp,)), dma((n_exp,)),
        ],
        compiler_params=pltpu.CompilerParams(
            collective_id=0, has_side_effects=True, vmem_limit_bytes=60 * 1024 * 1024
        ),
    )(grad_out, expert_ids, history_grad, history_hidden, down_weight)
    return out.reshape(1, 1, n_exp * capacity, units), new_g, new_h


def solution(mesh):
    in_specs = (
        P(("dp", "expert"), None),
        P(("dp", "expert"), None),
        P("expert", None, None),
        P(),
        P(),
    )
    out_specs = (P("dp", "expert", None, None), P(), P())
    return jax.shard_map(
        per_device, mesh=mesh, in_specs=in_specs, out_specs=out_specs, check_vma=False
    )
```

time: 113 us -> 68.5 us (0.61)
  Pallas kernels: 0 us -> 61.6 us
  waiting for transfers between devices: 45.2 us -> 0 us
  blocking collectives: 37.8 us -> 0 us
  matrix products: 8.85 us -> 0 us
  other arithmetic: 8.16 us -> 0 us
  starting transfers between devices: 6.49 us -> 0 us
  local copies, waits for them, and re-layouts: 4.51 us -> 5.97 us
    pallas_call x0 -> x1, Pallas kernels: none -> 61.6 us  [per_device(): pl.pallas_call(functools.partial(kernel, n_dp, n_exp, experts, capacity),...]
    all_to_all x1 -> x0, waiting for transfers between devices: 45.2 us -> none  [per_device(): lax.all_to_all(outgoing, 'expert', split_axis=0, concat_axis=0, tiled=True)]
    pmax x1 -> x0, blocking collectives: 37.8 us -> none  [per_device(): grad_amax, hidden_amax = lax.pmax((grad_peak, hidden_vec), ('dp', 'expert'))]
    dot_general x2 -> x0, matrix products: 8.85 us -> none  [the longest x1 7.11 us: per_device(): jnp.einsum('sic,uc->siu', received, weight_block, preferred_element_type=...]
    all_to_all x1 -> x0, starting transfers between devices: 6.49 us -> none  [per_device(): lax.all_to_all(outgoing, 'expert', split_axis=0, concat_axis=0, tiled=True)]
    convert_element_type x2 -> x0, other arithmetic: 3.85 us -> none  [the longest x1 3.85 us: per_device(): quantized = jnp.clip(gathered.reshape(experts, capacity, -1) * scale_in[:...]
    unnamed x9 -> x3, local copies, waits for them, and re-layouts: 0.8 us -> 3.95 us
    reduce_sum x4 -> x0, other arithmetic: 1.35 us -> none  [the longest x1 0.61 us: per_device(): own_scale_hidden = jnp.sum(jnp.where(chosen, scale_hidden, 0.0))]
  transfers between devices with their start and end apart: 1 -> 0, of which waited for: 1 -> 0; matrix products, arithmetic and copies ran while one was open for 1% -> 0% of each run, Pallas kernels for 0% -> 0%
where the time goes in v1:
time: 68.5 us; the launch traced here: 68.2 us
  Pallas kernels  61.6 us (90%)
  local copies, waits for them, and re-layouts  5.97 us (9%)
    pallas_call x1, Pallas kernels, per_device(): pl.pallas_call(functools.partial(kernel, n_dp, n_exp, experts, capacity),...  61.6 us
    unnamed x3, local copies, waits for them, and re-layouts  3.95 us
    reshape x1, local copies, waits for them, and re-layouts, per_device(): return (out.reshape(1, 1, n_exp * capacity, units), new_g, new_h)  2.01 us

profile of v1, /device:TPU:0, one launch (start us, length us, event | category | flops | bytes accessed | tf_op | source)
XLA Modules:
  0.0 68.2 jit_solution(13821491837076513906)
XLA Ops:
  0.6 1.4 %copy.9.ids_ref = s32[128,2]{1,0:T(8,128)} copy(s32[128,2]{0,1:T(2,128)} %param.6) | data formatting | bytes 2048 | tf_op args[1]
  2.0 61.6 %shard_map.76 = (bf16[8,36,1024]{2,1,0:T(8,128)(2,1)}, f32[8,8]{1,0:T(8,128)}, f32[8,8]{1,0:T(8,128)}) custom-call(bf16[128,3072]{1,0:T(8,128)(2,1)} %grad_ref.1, s32[128,2]{1,0:T(8,128)} %copy.9.ids_ref, f32[8,8]{1,0:T(8,128)} %hist_g_ref.1, f32[8,8]{1,0:T(8,128)} %hist_h_ref.1, bf16[1,1024,3072]{2,1,0:T(8,128)(2,1)} %weight_hbm.1), custom_call_target="tpu_custom_call" | custom-call | tf_op jit(solution)/shard_map/pallas_call | solution.py:226
  63.7 2.0 %reshape.9 = bf16[1,1,288,1024]{3,2,1,0:T(8,128)(2,1)} reshape(bf16[8,36,1024]{2,1,0:T(8,128)(2,1)} %get-tuple-element.6) | data formatting | bytes 1179648 | tf_op jit(solution)/shard_map/reshape | solution.py:250
  65.7 1.3 %copy.12 = f32[8,8]{1,0:T(8,128)} copy(f32[8,8]{1,0:T(8,128)} %get-tuple-element.13) | data formatting | bytes 512
  67.0 1.3 %copy.13 = f32[8,8]{1,0:T(8,128)} copy(f32[8,8]{1,0:T(8,128)} %get-tuple-element.14) | data formatting | bytes 512

commit v2 on v1

v2 whole, which is shorter than its diff:
```python
import functools

import jax
import jax.numpy as jnp
from jax import lax
from jax.experimental import pallas as pl
from jax.experimental.pallas import tpu as pltpu
from jax.sharding import PartitionSpec as P

MESH = pl.DeviceIdType.MESH
LANES = 128


def flip_bits(q, k, count):
    out, bit = 0, 1
    while bit < count:
        a, b = (q // bit) % 2, (k // bit) % 2
        out = out + bit * (a + b - 2 * a * b)
        bit *= 2
    return out


def kernel(
    n_dp, n_exp, experts, capacity,
    grad_ref, ids_ref, hist_g_ref, hist_h_ref, weight_hbm,
    out_ref, new_g_ref, new_h_ref,
    weight, send, send_rest, recv, recv_rest, rest_rows, slots, mine, peaks_in,
    weight_sem, send_sem, recv_sem, send_rest_sem, recv_rest_sem, peak_send_sem, peak_recv_sem,
):
    tokens = grad_ref.shape[0]
    main = send.shape[1]
    slices = n_exp // experts
    chips = n_exp // 2
    my_dp, me = lax.axis_index("dp"), lax.axis_index("expert")
    q0, c0 = me // 2, me % 2
    partner = q0 * 2 + 1 - c0
    own = me // slices
    load = pltpu.make_async_copy(weight_hbm.at[0], weight, weight_sem)
    load.start()

    barrier = pltpu.get_barrier_semaphore()

    everyone = n_dp * n_exp
    here = my_dp * n_exp + me

    def greet(j, x):
        peer = (here + j) % everyone
        pl.semaphore_signal(
            barrier, inc=1, device_id=(peer // n_exp, peer % n_exp), device_id_type=MESH
        )
        return x

    lax.fori_loop(1, everyone, greet, 0)

    expert_row = lax.broadcasted_iota(jnp.int32, (LANES, tokens), 0)
    ids = ids_ref[...]
    mask_t = jnp.where((ids[0:1, :] == expert_row) | (ids[1:2, :] == expert_row), 1.0, 0.0)
    row = lax.broadcasted_iota(jnp.int32, (tokens, tokens), 0)
    col = lax.broadcasted_iota(jnp.int32, (tokens, tokens), 1)
    earlier = jnp.where(row < col, 1.0, 0.0).astype(jnp.bfloat16)
    before = jnp.dot(mask_t.astype(jnp.bfloat16), earlier, preferred_element_type=jnp.float32)
    slots[...] = jnp.where(mask_t > 0.5, before, -1.0)
    scale_in = 1.0 / jnp.max(hist_g_ref[...], axis=0, keepdims=True)
    scale_hidden = 1.0 / jnp.max(hist_h_ref[...], axis=0, keepdims=True)
    which = lax.broadcasted_iota(jnp.int32, (1, experts), 1)

    def pick(values, e):
        return jnp.sum(jnp.where(which == e, values, 0.0), axis=1, keepdims=True)

    position = lax.broadcasted_iota(jnp.int32, (capacity, tokens), 0).astype(jnp.float32)

    def prepare(e):
        onehot = jnp.where(slots[pl.ds(e, 1), :] == position, 1.0, 0.0).astype(jnp.bfloat16)
        rows = jnp.dot(onehot, grad_ref[...], preferred_element_type=jnp.float32)
        block = jnp.clip(rows * pick(scale_in, e), -1.0, 1.0)
        send[e] = block[0:main].astype(jnp.bfloat16)
        send_rest[e] = block[main:capacity].astype(jnp.bfloat16)

    def outgoing(d):
        return pltpu.make_async_remote_copy(
            src_ref=send.at[d // slices], dst_ref=recv.at[me],
            send_sem=send_sem.at[d], recv_sem=recv_sem.at[me],
            device_id=(my_dp, d), device_id_type=MESH,
        )

    def outgoing_rest(d):
        return pltpu.make_async_remote_copy(
            src_ref=send_rest.at[d // slices], dst_ref=recv_rest.at[me],
            send_sem=send_rest_sem.at[d], recv_sem=recv_rest_sem.at[me],
            device_id=(my_dp, d), device_id_type=MESH,
        )

    def incoming(s):
        return pltpu.make_async_remote_copy(
            src_ref=send.at[0], dst_ref=recv.at[s],
            send_sem=send_sem.at[s], recv_sem=recv_sem.at[s],
            device_id=(my_dp, s), device_id_type=MESH,
        )

    def incoming_rest(s):
        return pltpu.make_async_remote_copy(
            src_ref=send_rest.at[0], dst_ref=recv_rest.at[s],
            send_sem=send_rest_sem.at[s], recv_sem=recv_rest_sem.at[s],
            device_id=(my_dp, s), device_id_type=MESH,
        )

    def chip_of(j):
        k = jnp.where(j < 2, j, chips + 1 - j)
        if chips & (chips - 1) == 0:
            return flip_bits(q0, k, chips)
        return (q0 + k) % chips

    def source_of(j):
        if chips & (chips - 1) == 0:
            return chip_of(j)
        k = jnp.where(j < 2, j, chips + 1 - j)
        return (q0 + chips - k) % chips

    def prepare_pair(q):
        prepare(2 * q + c0)
        prepare(2 * q + 1 - c0)

    def send_pair(q):
        for c in (c0, 1 - c0):
            outgoing(2 * q + c).start()
            outgoing_rest(2 * q + c).start()

    greeted = everyone - 1
    if slices == 1:
        prepare_pair(chip_of(jnp.int32(1)))
        pl.semaphore_wait(barrier, greeted)

        def step(j, x):
            prepare_pair(chip_of((j + 1) % chips))
            send_pair(chip_of(j))
            return x
    else:
        def fill(e, x):
            prepare(e)
            return x

        lax.fori_loop(0, experts, fill, 0)
        pl.semaphore_wait(barrier, greeted)

        def step(j, x):
            send_pair(chip_of(j))
            return x

    lax.fori_loop(1, chips, step, 0)
    outgoing(partner).start()
    outgoing_rest(partner).start()

    recv[me] = send[own]
    recv_rest[me] = send_rest[own]
    row_peak = jnp.max(jnp.abs(grad_ref[...]).astype(jnp.float32), axis=1, keepdims=True)
    grad_peak = jnp.max(jnp.where(mask_t.T > 0.5, row_peak, 0.0), axis=0, keepdims=True)

    back = 1.0 / pick(scale_in, own)
    own_hidden = pick(scale_hidden, own)
    load.wait()

    def multiply(block):
        product = lax.dot_general(
            block, weight[...], (((1,), (1,)), ((), ())), preferred_element_type=jnp.float32
        )
        hidden = product * back
        scaled = jnp.clip(hidden * own_hidden, -1.0, 1.0)
        return scaled, jnp.max(jnp.max(jnp.abs(hidden), axis=0, keepdims=True), axis=1, keepdims=True)

    def pair_rows(q):
        return recv[pl.ds(2 * q, 2)].reshape(2 * main, recv.shape[2])

    def put_pair(q, scaled):
        for c in range(2):
            out_ref[2 * q + c, 0:main, :] = scaled[c * main:(c + 1) * main].astype(jnp.bfloat16)

    def take_own():
        incoming(partner).wait_recv()
        scaled, peak = multiply(pair_rows(q0))
        put_pair(q0, scaled)
        return peak

    def take(j, peak):
        q = source_of(j)
        incoming(2 * q).wait_recv()
        incoming(2 * q + 1).wait_recv()
        scaled, peak_here = multiply(pair_rows(q))
        put_pair(q, scaled)
        return jnp.maximum(peak, peak_here)

    peak = lax.fori_loop(1, chips - 1, take, take_own())

    def take_rest(j, x):
        incoming_rest((me + j) % n_exp).wait_recv()
        return x

    lax.fori_loop(1, n_exp, take_rest, 0)
    rest = capacity - main
    for s in range(n_exp):
        rest_rows[s * rest:(s + 1) * rest, :] = recv_rest[s].astype(jnp.float32)
    last = source_of(jnp.int32(chips - 1))
    incoming(2 * last).wait_recv()
    incoming(2 * last + 1).wait_recv()
    block = jnp.concatenate([pair_rows(last), rest_rows[...].astype(jnp.bfloat16)], axis=0)
    scaled, peak_here = multiply(block)
    peak = jnp.maximum(peak, peak_here)

    at = lax.broadcasted_iota(jnp.int32, (1, LANES), 1)
    hidden_peak = jnp.where(at == own, peak, 0.0)
    part = lax.broadcasted_iota(jnp.int32, (8, LANES), 0)
    mine[...] = jnp.where(part == 0, grad_peak, jnp.where(part == 1, hidden_peak, 0.0))

    def peak_copy(peer, slot, j):
        return pltpu.make_async_remote_copy(
            src_ref=mine, dst_ref=peaks_in.at[slot],
            send_sem=peak_send_sem.at[j], recv_sem=peak_recv_sem.at[slot],
            device_id=(peer // n_exp, peer % n_exp), device_id_type=MESH,
        )

    def peak_start(j, x):
        peak_copy((here + j) % everyone, here, j).start()
        return x

    def peak_fold(j, best):
        peer = (here + j) % everyone
        peak_copy(peer, peer, j).wait_recv()
        return jnp.maximum(best, peaks_in[peer])

    def peak_finish(j, x):
        peak_copy((here + j) % everyone, here, j).wait_send()
        return x

    lax.fori_loop(1, everyone, peak_start, 0)
    put_pair(last, scaled)
    for s in range(n_exp):
        at_row = 2 * main + s * rest
        out_ref[s, main:capacity, :] = scaled[at_row:at_row + rest].astype(jnp.bfloat16)
    best = lax.fori_loop(1, everyone, peak_fold, mine[...])
    lax.fori_loop(1, everyone, peak_finish, 0)

    keep = hist_g_ref.shape[0] - 1
    new_g_ref[0:keep, :] = hist_g_ref[1:keep + 1, :]
    new_g_ref[keep:keep + 1, :] = best[0:1, 0:experts]
    new_h_ref[0:keep, :] = hist_h_ref[1:keep + 1, :]
    new_h_ref[keep:keep + 1, :] = best[1:2, 0:experts]

    def drain(j, x):
        outgoing((me + j) % n_exp).wait_send()
        outgoing_rest((me + j) % n_exp).wait_send()
        return x

    lax.fori_loop(1, n_exp, drain, 0)


def per_device(grad_out, expert_ids, down_weight, history_grad, history_hidden):
    tokens, width = grad_out.shape
    experts = history_grad.shape[1]
    n_dp, n_exp = lax.axis_size("dp"), lax.axis_size("expert")
    capacity = tokens * 9 // 32
    main = (capacity - 1) // 16 * 16
    rest = capacity - main
    units = down_weight.shape[1]
    vmem = pl.BlockSpec(memory_space=pltpu.VMEM)
    dma = pltpu.SemaphoreType.DMA
    out, new_g, new_h = pl.pallas_call(
        functools.partial(kernel, n_dp, n_exp, experts, capacity),
        out_shape=(
            jax.ShapeDtypeStruct((n_exp, capacity, units), jnp.bfloat16),
            jax.ShapeDtypeStruct(history_grad.shape, jnp.float32),
            jax.ShapeDtypeStruct(history_hidden.shape, jnp.float32),
        ),
        in_specs=[vmem, vmem, vmem, vmem, pl.BlockSpec(memory_space=pl.ANY)],
        out_specs=(vmem, vmem, vmem),
        scratch_shapes=[
            pltpu.VMEM((units, width), jnp.bfloat16),
            pltpu.VMEM((experts, main, width), jnp.bfloat16),
            pltpu.VMEM((experts, rest, width), jnp.bfloat16),
            pltpu.VMEM((n_exp, main, width), jnp.bfloat16),
            pltpu.VMEM((n_exp, rest, width), jnp.bfloat16),
            pltpu.VMEM((n_exp * rest, width), jnp.float32),
            pltpu.VMEM((LANES, tokens), jnp.float32),
            pltpu.VMEM((8, LANES), jnp.float32),
            pltpu.VMEM((n_dp * n_exp, 8, LANES), jnp.float32),
            dma, dma((n_exp,)), dma((n_exp,)), dma((n_exp,)), dma((n_exp,)),
            dma((n_dp * n_exp,)), dma((n_dp * n_exp,)),
        ],
        compiler_params=pltpu.CompilerParams(
            collective_id=0, has_side_effects=True, vmem_limit_bytes=60 * 1024 * 1024
        ),
    )(grad_out, expert_ids.T, history_grad, history_hidden, down_weight)
    return out.reshape(1, 1, n_exp * capacity, units), new_g, new_h


def solution(mesh):
    in_specs = (
        P(("dp", "expert"), None),
        P(("dp", "expert"), None),
        P("expert", None, None),
        P(),
        P(),
    )
    out_specs = (P("dp", "expert", None, None), P(), P())
    return jax.shard_map(
        per_device, mesh=mesh, in_specs=in_specs, out_specs=out_specs, check_vma=False
    )
```

time: 68.5 us -> 63.6 us (0.928)
  Pallas kernels: 61.6 us -> 58.1 us
  local copies, waits for them, and re-layouts: 5.97 us -> 4.55 us
    pallas_call x1, Pallas kernels: 61.6 us -> 58.1 us  [per_device(): pl.pallas_call(functools.partial(kernel, n_dp, n_exp, experts, capacity),...]
    unnamed x3 -> x2, local copies, waits for them, and re-layouts: 3.95 us -> 2.54 us
where the time goes in v2:
time: 63.6 us; the launch traced here: 63.3 us
  Pallas kernels  58.1 us (91%)
  local copies, waits for them, and re-layouts  4.55 us (7%)
  between operations  0.64 us (1%)
    pallas_call x1, Pallas kernels, per_device(): pl.pallas_call(functools.partial(kernel, n_dp, n_exp, experts, capacity),...  58.1 us
    unnamed x2, local copies, waits for them, and re-layouts  2.54 us
    reshape x1, local copies, waits for them, and re-layouts, per_device(): return (out.reshape(1, 1, n_exp * capacity, units), new_g, new_h)  2.01 us

profile of v2, /device:TPU:0, one launch (start us, length us, event | category | flops | bytes accessed | tf_op | source)
XLA Modules:
  0.0 63.3 jit_solution(4388730766906008367)
XLA Ops:
  0.6 58.1 %shard_map.76 = (bf16[8,36,1024]{2,1,0:T(8,128)(2,1)}, f32[8,8]{1,0:T(8,128)}, f32[8,8]{1,0:T(8,128)}) custom-call(bf16[128,3072]{1,0:T(8,128)(2,1)} %grad_ref.1, s32[2,128]{1,0:T(2,128)} %bitcast.1, f32[8,8]{1,0:T(8,128)} %hist_g_ref.1, f32[8,8]{1,0:T(8,128)} %hist_h_ref.1, bf16[1,1024,3072]{2,1,0:T(8,128)(2,1)} %weight_hbm.1), custom_call_target="tpu_custom_call" | custom-call | tf_op jit(solution)/shard_map/pallas_call | solution.py:265
  58.8 2.0 %reshape.9 = bf16[1,1,288,1024]{3,2,1,0:T(8,128)(2,1)} reshape(bf16[8,36,1024]{2,1,0:T(8,128)(2,1)} %get-tuple-element.6) | data formatting | bytes 1179648 | tf_op jit(solution)/shard_map/reshape | solution.py:291
  60.8 1.3 %copy.10 = f32[8,8]{1,0:T(8,128)} copy(f32[8,8]{1,0:T(8,128)} %get-tuple-element.13) | data formatting | bytes 512
  62.1 1.3 %copy.11 = f32[8,8]{1,0:T(8,128)} copy(f32[8,8]{1,0:T(8,128)} %get-tuple-element.14) | data formatting | bytes 512

commit v3 on v2

--- a/solution.py
+++ b/solution.py
@@ -23,8 +23,8 @@
 def kernel(
     n_dp, n_exp, experts, capacity,
     grad_ref, ids_ref, hist_g_ref, hist_h_ref, weight_hbm,
-    out_ref, new_g_ref, new_h_ref,
-    weight, send, send_rest, recv, recv_rest, rest_rows, slots, mine, peaks_in,
+    out_ref, best_ref,
+    held, weight, send, send_rest, recv, recv_rest, rest_rows, slots, mine, peaks_in,
     weight_sem, send_sem, recv_sem, send_rest_sem, recv_rest_sem, peak_send_sem, peak_recv_sem,
 ):
     tokens = grad_ref.shape[0]
@@ -105,7 +105,7 @@
         )
 
     def chip_of(j):
-        k = jnp.where(j < 2, j, chips + 1 - j)
+        k = j
         if chips & (chips - 1) == 0:
             return flip_bits(q0, k, chips)
         return (q0 + k) % chips
@@ -113,7 +113,7 @@
     def source_of(j):
         if chips & (chips - 1) == 0:
             return chip_of(j)
-        k = jnp.where(j < 2, j, chips + 1 - j)
+        k = j
         return (q0 + chips - k) % chips
 
     def prepare_pair(q):
@@ -172,7 +172,7 @@
 
     def put_pair(q, scaled):
         for c in range(2):
-            out_ref[2 * q + c, 0:main, :] = scaled[c * main:(c + 1) * main].astype(jnp.bfloat16)
+            held[2 * q + c] = scaled[c * main:(c + 1) * main].astype(jnp.bfloat16)
 
     def take_own():
         incoming(partner).wait_recv()
@@ -234,15 +234,13 @@
     put_pair(last, scaled)
     for s in range(n_exp):
         at_row = 2 * main + s * rest
-        out_ref[s, main:capacity, :] = scaled[at_row:at_row + rest].astype(jnp.bfloat16)
+        base = s * capacity
+        out_ref[base:base + main, :] = held[s]
+        out_ref[base + main:base + capacity, :] = scaled[at_row:at_row + rest].astype(jnp.bfloat16)
     best = lax.fori_loop(1, everyone, peak_fold, mine[...])
     lax.fori_loop(1, everyone, peak_finish, 0)
 
-    keep = hist_g_ref.shape[0] - 1
-    new_g_ref[0:keep, :] = hist_g_ref[1:keep + 1, :]
-    new_g_ref[keep:keep + 1, :] = best[0:1, 0:experts]
-    new_h_ref[0:keep, :] = hist_h_ref[1:keep + 1, :]
-    new_h_ref[keep:keep + 1, :] = best[1:2, 0:experts]
+    best_ref[...] = best
 
     def drain(j, x):
         outgoing((me + j) % n_exp).wait_send()
@@ -250,6 +248,16 @@
         return x
 
     lax.fori_loop(1, n_exp, drain, 0)
+
+
+def finish_kernel(hist_g_ref, hist_h_ref, best_ref, out_ref, new_g_ref, new_h_ref, final_ref):
+    final_ref[...] = out_ref[...]
+    keep = hist_g_ref.shape[0] - 1
+    experts = hist_g_ref.shape[1]
+    new_g_ref[0:keep, :] = hist_g_ref[1:keep + 1, :]
+    new_g_ref[keep:keep + 1, :] = best_ref[0:1, 0:experts]
+    new_h_ref[0:keep, :] = hist_h_ref[1:keep + 1, :]
+    new_h_ref[keep:keep + 1, :] = best_ref[1:2, 0:experts]
 
 
 def per_device(grad_out, expert_ids, down_weight, history_grad, history_hidden):
@@ -262,16 +270,16 @@
     units = down_weight.shape[1]
     vmem = pl.BlockSpec(memory_space=pltpu.VMEM)
     dma = pltpu.SemaphoreType.DMA
-    out, new_g, new_h = pl.pallas_call(
+    out, best = pl.pallas_call(
         functools.partial(kernel, n_dp, n_exp, experts, capacity),
         out_shape=(
-            jax.ShapeDtypeStruct((n_exp, capacity, units), jnp.bfloat16),
-            jax.ShapeDtypeStruct(history_grad.shape, jnp.float32),
-            jax.ShapeDtypeStruct(history_hidden.shape, jnp.float32),
+            jax.ShapeDtypeStruct((n_exp * capacity, units), jnp.bfloat16),
+            jax.ShapeDtypeStruct((8, LANES), jnp.float32),
         ),
         in_specs=[vmem, vmem, vmem, vmem, pl.BlockSpec(memory_space=pl.ANY)],
-        out_specs=(vmem, vmem, vmem),
+        out_specs=(vmem, vmem),
         scratch_shapes=[
+            pltpu.VMEM((n_exp, main, units), jnp.bfloat16),
             pltpu.VMEM((units, width), jnp.bfloat16),
             pltpu.VMEM((experts, main, width), jnp.bfloat16),
             pltpu.VMEM((experts, rest, width), jnp.bfloat16),
@@ -288,6 +296,16 @@
             collective_id=0, has_side_effects=True, vmem_limit_bytes=60 * 1024 * 1024
         ),
     )(grad_out, expert_ids.T, history_grad, history_hidden, down_weight)
+    new_g, new_h, out = pl.pallas_call(
+        finish_kernel,
+        out_shape=(
+            jax.ShapeDtypeStruct(history_grad.shape, jnp.float32),
+            jax.ShapeDtypeStruct(history_hidden.shape, jnp.float32),
+            jax.ShapeDtypeStruct(out.shape, out.dtype),
+        ),
+        in_specs=[vmem, vmem, vmem, vmem],
+        out_specs=(vmem, vmem, vmem),
+    )(history_grad, history_hidden, best, out)
     return out.reshape(1, 1, n_exp * capacity, units), new_g, new_h
 
 

time: 63.6 us -> 60.5 us (0.951)
  local copies, waits for them, and re-layouts: 4.55 us -> 0 us
  Pallas kernels: 58.1 us -> 59.7 us
    unnamed x2 -> x0, local copies, waits for them, and re-layouts: 2.54 us -> none
    reshape x1 -> x0, local copies, waits for them, and re-layouts: 2.01 us -> none  [per_device(): return (out.reshape(1, 1, n_exp * capacity, units), new_g, new_h)]
    pallas_call x0 -> x1, Pallas kernels: none -> 1.96 us  [per_device(): pl.pallas_call(finish_kernel, out_shape=(jax.ShapeDtypeStruct(history_gra...]
where the time goes in v3:
time: 60.5 us; the launch traced here: 60.3 us
  Pallas kernels  59.7 us (99%)
  between operations  0.64 us (1%)
    pallas_call x1, Pallas kernels, per_device(): pl.pallas_call(functools.partial(kernel, n_dp, n_exp, experts, capacity),...  57.7 us
    pallas_call x1, Pallas kernels, per_device(): pl.pallas_call(finish_kernel, out_shape=(jax.ShapeDtypeStruct(history_gra...  1.96 us

profile of v3, /device:TPU:0, one launch (start us, length us, event | category | flops | bytes accessed | tf_op | source)
XLA Modules:
  0.0 60.3 jit_solution(16801554326775227622)
XLA Ops:
  0.6 57.7 %shard_map.76 = (bf16[288,1024]{1,0:T(8,128)(2,1)}, f32[8,128]{1,0:T(8,128)}) custom-call(bf16[128,3072]{1,0:T(8,128)(2,1)} %grad_ref.1, s32[2,128]{1,0:T(2,128)} %bitcast.2, f32[8,8]{1,0:T(8,128)} %hist_g_ref.3, f32[8,8]{1,0:T(8,128)} %hist_h_ref.3, bf16[1,1024,3072]{2,1,0:T(8,128)(2,1)} %weight_hbm.1), custom_call_target="tpu_custom_call" | custom-call | tf_op jit(solution)/shard_map/pallas_call | solution.py:273
  58.3 2.0 %shard_map.77 = (f32[8,8]{1,0:T(8,128)}, f32[8,8]{1,0:T(8,128)}, bf16[288,1024]{1,0:T(8,128)(2,1)}) custom-call(f32[8,8]{1,0:T(8,128)} %hist_g_ref.3, f32[8,8]{1,0:T(8,128)} %hist_h_ref.3, f32[8,128]{1,0:T(8,128)} %get-tuple-element.8.best_ref, bf16[288,1024]{1,0:T(8,128)(2,1)} %get-tuple-element.9.out_ref), custom_call_target="tpu_custom_call" | custom-call | tf_op jit(solution)/shard_map/pallas_call | solution.py:299

commit v4 on v3

--- a/solution.py
+++ b/solution.py
@@ -8,6 +8,7 @@
 from jax.sharding import PartitionSpec as P
 
 MESH = pl.DeviceIdType.MESH
+PARTS = 4
 LANES = 128
 
 
@@ -76,10 +77,13 @@
         send[e] = block[0:main].astype(jnp.bfloat16)
         send_rest[e] = block[main:capacity].astype(jnp.bfloat16)
 
-    def outgoing(d):
-        return pltpu.make_async_remote_copy(
-            src_ref=send.at[d // slices], dst_ref=recv.at[me],
-            send_sem=send_sem.at[d], recv_sem=recv_sem.at[me],
+    span = weight.shape[1] // PARTS
+
+    def outgoing(d, p):
+        columns = pl.ds(p * span, span)
+        return pltpu.make_async_remote_copy(
+            src_ref=send.at[d // slices, :, columns], dst_ref=recv.at[me, :, columns],
+            send_sem=send_sem.at[p, d], recv_sem=recv_sem.at[p, me],
             device_id=(my_dp, d), device_id_type=MESH,
         )
 
@@ -90,10 +94,11 @@
             device_id=(my_dp, d), device_id_type=MESH,
         )
 
-    def incoming(s):
-        return pltpu.make_async_remote_copy(
-            src_ref=send.at[0], dst_ref=recv.at[s],
-            send_sem=send_sem.at[s], recv_sem=recv_sem.at[s],
+    def incoming(s, p):
+        columns = pl.ds(p * span, span)
+        return pltpu.make_async_remote_copy(
+            src_ref=send.at[0, :, columns], dst_ref=recv.at[s, :, columns],
+            send_sem=send_sem.at[p, s], recv_sem=recv_sem.at[p, s],
             device_id=(my_dp, s), device_id_type=MESH,
         )
 
@@ -121,9 +126,11 @@
         prepare(2 * q + 1 - c0)
 
     def send_pair(q):
-        for c in (c0, 1 - c0):
-            outgoing(2 * q + c).start()
-            outgoing_rest(2 * q + c).start()
+        for p in range(PARTS):
+            for c in (c0, 1 - c0):
+                outgoing(2 * q + c, p).start()
+                if p == 0:
+                    outgoing_rest(2 * q + c).start()
 
     greeted = everyone - 1
     if slices == 1:
@@ -147,7 +154,8 @@
             return x
 
     lax.fori_loop(1, chips, step, 0)
-    outgoing(partner).start()
+    for p in range(PARTS):
+        outgoing(partner, p).start()
     outgoing_rest(partner).start()
 
     recv[me] = send[own]
@@ -159,10 +167,15 @@
     own_hidden = pick(scale_hidden, own)
     load.wait()
 
+    def times_weight(block, columns):
+        return lax.dot_general(
+            block, weight[:, columns], (((1,), (1,)), ((), ())), preferred_element_type=jnp.float32
+        )
+
     def multiply(block):
-        product = lax.dot_general(
-            block, weight[...], (((1,), (1,)), ((), ())), preferred_element_type=jnp.float32
-        )
+        return finish(times_weight(block, slice(None)))
+
+    def finish(product):
         hidden = product * back
         scaled = jnp.clip(hidden * own_hidden, -1.0, 1.0)
         return scaled, jnp.max(jnp.max(jnp.abs(hidden), axis=0, keepdims=True), axis=1, keepdims=True)
@@ -175,15 +188,17 @@
             held[2 * q + c] = scaled[c * main:(c + 1) * main].astype(jnp.bfloat16)
 
     def take_own():
-        incoming(partner).wait_recv()
+        for p in range(PARTS):
+            incoming(partner, p).wait_recv()
         scaled, peak = multiply(pair_rows(q0))
         put_pair(q0, scaled)
         return peak
 
     def take(j, peak):
         q = source_of(j)
-        incoming(2 * q).wait_recv()
-        incoming(2 * q + 1).wait_recv()
+        for p in range(PARTS):
+            incoming(2 * q, p).wait_recv()
+            incoming(2 * q + 1, p).wait_recv()
         scaled, peak_here = multiply(pair_rows(q))
         put_pair(q, scaled)
         return jnp.maximum(peak, peak_here)
@@ -199,10 +214,16 @@
     for s in range(n_exp):
         rest_rows[s * rest:(s + 1) * rest, :] = recv_rest[s].astype(jnp.float32)
     last = source_of(jnp.int32(chips - 1))
-    incoming(2 * last).wait_recv()
-    incoming(2 * last + 1).wait_recv()
-    block = jnp.concatenate([pair_rows(last), rest_rows[...].astype(jnp.bfloat16)], axis=0)
-    scaled, peak_here = multiply(block)
+    product = None
+    for p in range(PARTS):
+        incoming(2 * last, p).wait_recv()
+        incoming(2 * last + 1, p).wait_recv()
+        columns = slice(p * span, (p + 1) * span)
+        pair = recv[pl.ds(2 * last, 2), :, columns].reshape(2 * main, span)
+        block = jnp.concatenate([pair, rest_rows[:, columns].astype(jnp.bfloat16)], axis=0)
+        piece = times_weight(block, columns)
+        product = piece if product is None else product + piece
+    scaled, peak_here = finish(product)
     peak = jnp.maximum(peak, peak_here)
 
     at = lax.broadcasted_iota(jnp.int32, (1, LANES), 1)
@@ -243,7 +264,8 @@
     best_ref[...] = best
 
     def drain(j, x):
-        outgoing((me + j) % n_exp).wait_send()
+        for p in range(PARTS):
+            outgoing((me + j) % n_exp, p).wait_send()
         outgoing_rest((me + j) % n_exp).wait_send()
         return x
 
@@ -289,7 +311,7 @@
             pltpu.VMEM((LANES, tokens), jnp.float32),
             pltpu.VMEM((8, LANES), jnp.float32),
             pltpu.VMEM((n_dp * n_exp, 8, LANES), jnp.float32),
-            dma, dma((n_exp,)), dma((n_exp,)), dma((n_exp,)), dma((n_exp,)),
+            dma, dma((PARTS, n_exp)), dma((PARTS, n_exp)), dma((n_exp,)), dma((n_exp,)),
             dma((n_dp * n_exp,)), dma((n_dp * n_exp,)),
         ],
         compiler_params=pltpu.CompilerParams(

time: 60.5 us -> 59.5 us (0.983)
  Pallas kernels: 59.7 us -> 58.7 us
    pallas_call x1, Pallas kernels: 57.7 us -> 56.7 us  [per_device(): pl.pallas_call(functools.partial(kernel, n_dp, n_exp, experts, capacity),...]
where the time goes in v4:
time: 59.5 us; the launch traced here: 59.3 us
  Pallas kernels  58.7 us (99%)
  between operations  0.64 us (1%)
    pallas_call x1, Pallas kernels, per_device(): pl.pallas_call(functools.partial(kernel, n_dp, n_exp, experts, capacity),...  56.7 us
    pallas_call x1, Pallas kernels, per_device(): pl.pallas_call(finish_kernel, out_shape=(jax.ShapeDtypeStruct(history_gra...  1.96 us

profile of v4, /device:TPU:0, one launch (start us, length us, event | category | flops | bytes accessed | tf_op | source)
XLA Modules:
  0.0 59.3 jit_solution(8176014672207970862)
XLA Ops:
  0.6 56.7 %shard_map.76 = (bf16[288,1024]{1,0:T(8,128)(2,1)}, f32[8,128]{1,0:T(8,128)}) custom-call(bf16[128,3072]{1,0:T(8,128)(2,1)} %grad_ref.1, s32[2,128]{1,0:T(2,128)} %bitcast.2, f32[8,8]{1,0:T(8,128)} %hist_g_ref.3, f32[8,8]{1,0:T(8,128)} %hist_h_ref.3, bf16[1,1024,3072]{2,1,0:T(8,128)(2,1)} %weight_hbm.1), custom_call_target="tpu_custom_call" | custom-call | tf_op jit(solution)/shard_map/pallas_call | solution.py:295
  57.4 2.0 %shard_map.77 = (f32[8,8]{1,0:T(8,128)}, f32[8,8]{1,0:T(8,128)}, bf16[288,1024]{1,0:T(8,128)(2,1)}) custom-call(f32[8,8]{1,0:T(8,128)} %hist_g_ref.3, f32[8,8]{1,0:T(8,128)} %hist_h_ref.3, f32[8,128]{1,0:T(8,128)} %get-tuple-element.8.best_ref, bf16[288,1024]{1,0:T(8,128)(2,1)} %get-tuple-element.9.out_ref), custom_call_target="tpu_custom_call" | custom-call | tf_op jit(solution)/shard_map/pallas_call | solution.py:321

commit v5 on v4

--- a/solution.py
+++ b/solution.py
@@ -23,10 +23,10 @@
 
 def kernel(
     n_dp, n_exp, experts, capacity,
-    grad_ref, ids_ref, hist_g_ref, hist_h_ref, weight_hbm,
+    grad_hbm, ids_ref, hist_g_ref, hist_h_ref, weight_hbm,
     out_ref, best_ref,
-    held, weight, send, send_rest, recv, recv_rest, rest_rows, slots, mine, peaks_in,
-    weight_sem, send_sem, recv_sem, send_rest_sem, recv_rest_sem, peak_send_sem, peak_recv_sem,
+    grad_ref, held, weight, send, send_rest, recv, recv_rest, rest_rows, slots, mine, peaks_in,
+    grad_sem, weight_sem, send_sem, recv_sem, send_rest_sem, recv_rest_sem, peak_send_sem, peak_recv_sem,
 ):
     tokens = grad_ref.shape[0]
     main = send.shape[1]
@@ -36,8 +36,9 @@
     q0, c0 = me // 2, me % 2
     partner = q0 * 2 + 1 - c0
     own = me // slices
+    grad_load = pltpu.make_async_copy(grad_hbm, grad_ref, grad_sem)
+    grad_load.start()
     load = pltpu.make_async_copy(weight_hbm.at[0], weight, weight_sem)
-    load.start()
 
     barrier = pltpu.get_barrier_semaphore()
 
@@ -133,6 +134,8 @@
                     outgoing_rest(2 * q + c).start()
 
     greeted = everyone - 1
+    grad_load.wait()
+    load.start()
     if slices == 1:
         prepare_pair(chip_of(jnp.int32(1)))
         pl.semaphore_wait(barrier, greeted)
@@ -298,9 +301,10 @@
             jax.ShapeDtypeStruct((n_exp * capacity, units), jnp.bfloat16),
             jax.ShapeDtypeStruct((8, LANES), jnp.float32),
         ),
-        in_specs=[vmem, vmem, vmem, vmem, pl.BlockSpec(memory_space=pl.ANY)],
+        in_specs=[pl.BlockSpec(memory_space=pl.ANY), vmem, vmem, vmem, pl.BlockSpec(memory_space=pl.ANY)],
         out_specs=(vmem, vmem),
         scratch_shapes=[
+            pltpu.VMEM((tokens, width), jnp.bfloat16),
             pltpu.VMEM((n_exp, main, units), jnp.bfloat16),
             pltpu.VMEM((units, width), jnp.bfloat16),
             pltpu.VMEM((experts, main, width), jnp.bfloat16),
@@ -311,7 +315,7 @@
             pltpu.VMEM((LANES, tokens), jnp.float32),
             pltpu.VMEM((8, LANES), jnp.float32),
             pltpu.VMEM((n_dp * n_exp, 8, LANES), jnp.float32),
-            dma, dma((PARTS, n_exp)), dma((PARTS, n_exp)), dma((n_exp,)), dma((n_exp,)),
+            dma, dma, dma((PARTS, n_exp)), dma((PARTS, n_exp)), dma((n_exp,)), dma((n_exp,)),
             dma((n_dp * n_exp,)), dma((n_dp * n_exp,)),
         ],
         compiler_params=pltpu.CompilerParams(

time: 59.5 us -> 59.1 us (level)
  no operation moved by 1% of the time
where the time goes in v5:
time: 59.1 us; the launch traced here: 58.9 us
  Pallas kernels  58.3 us (99%)
  between operations  0.64 us (1%)
    pallas_call x1, Pallas kernels, per_device(): pl.pallas_call(functools.partial(kernel, n_dp, n_exp, experts, capacity),...  56.3 us
    pallas_call x1, Pallas kernels, per_device(): pl.pallas_call(finish_kernel, out_shape=(jax.ShapeDtypeStruct(history_gra...  1.96 us

profile of v5, /device:TPU:0, one launch (start us, length us, event | category | flops | bytes accessed | tf_op | source)
XLA Modules:
  0.0 58.9 jit_solution(12801691303779879993)
XLA Ops:
  0.6 56.3 %shard_map.76 = (bf16[288,1024]{1,0:T(8,128)(2,1)}, f32[8,128]{1,0:T(8,128)}) custom-call(bf16[128,3072]{1,0:T(8,128)(2,1)} %grad_hbm.1, s32[2,128]{1,0:T(2,128)} %bitcast.2, f32[8,8]{1,0:T(8,128)} %hist_g_ref.3, f32[8,8]{1,0:T(8,128)} %hist_h_ref.3, bf16[1,1024,3072]{2,1,0:T(8,128)(2,1)} %weight_hbm.1), custom_call_target="tpu_custom_call" | custom-call | tf_op jit(solution)/shard_map/pallas_call | solution.py:298
  57.0 2.0 %shard_map.77 = (f32[8,8]{1,0:T(8,128)}, f32[8,8]{1,0:T(8,128)}, bf16[288,1024]{1,0:T(8,128)(2,1)}) custom-call(f32[8,8]{1,0:T(8,128)} %hist_g_ref.3, f32[8,8]{1,0:T(8,128)} %hist_h_ref.3, f32[8,128]{1,0:T(8,128)} %get-tuple-element.8.best_ref, bf16[288,1024]{1,0:T(8,128)(2,1)} %get-tuple-element.9.out_ref), custom_call_target="tpu_custom_call" | custom-call | tf_op jit(solution)/shard_map/pallas_call | solution.py:325

commit v6 on v5

--- a/solution.py
+++ b/solution.py
@@ -8,7 +8,7 @@
 from jax.sharding import PartitionSpec as P
 
 MESH = pl.DeviceIdType.MESH
-PARTS = 4
+PARTS = 6
 LANES = 128
 
 

time: 59.1 us -> 59.4 us (level)
  no operation moved by 1% of the time
where the time goes in v6:
time: 59.4 us; the launch traced here: 59.1 us
  Pallas kernels  58.5 us (98%)
  between operations  0.64 us (1%)
    pallas_call x1, Pallas kernels, per_device(): pl.pallas_call(functools.partial(kernel, n_dp, n_exp, experts, capacity),...  56.5 us
    pallas_call x1, Pallas kernels, per_device(): pl.pallas_call(finish_kernel, out_shape=(jax.ShapeDtypeStruct(history_gra...  1.96 us

profile of v6, /device:TPU:0, one launch (start us, length us, event | category | flops | bytes accessed | tf_op | source)
XLA Modules:
  0.0 59.1 jit_solution(16088669611683454648)
XLA Ops:
  0.6 56.5 %shard_map.76 = (bf16[288,1024]{1,0:T(8,128)(2,1)}, f32[8,128]{1,0:T(8,128)}) custom-call(bf16[128,3072]{1,0:T(8,128)(2,1)} %grad_hbm.1, s32[2,128]{1,0:T(2,128)} %bitcast.2, f32[8,8]{1,0:T(8,128)} %hist_g_ref.3, f32[8,8]{1,0:T(8,128)} %hist_h_ref.3, bf16[1,1024,3072]{2,1,0:T(8,128)(2,1)} %weight_hbm.1), custom_call_target="tpu_custom_call" | custom-call | tf_op jit(solution)/shard_map/pallas_call | solution.py:298
  57.1 2.0 %shard_map.77 = (f32[8,8]{1,0:T(8,128)}, f32[8,8]{1,0:T(8,128)}, bf16[288,1024]{1,0:T(8,128)(2,1)}) custom-call(f32[8,8]{1,0:T(8,128)} %hist_g_ref.3, f32[8,8]{1,0:T(8,128)} %hist_h_ref.3, f32[8,128]{1,0:T(8,128)} %get-tuple-element.8.best_ref, bf16[288,1024]{1,0:T(8,128)(2,1)} %get-tuple-element.9.out_ref), custom_call_target="tpu_custom_call" | custom-call | tf_op jit(solution)/shard_map/pallas_call | solution.py:325
